TPU v7x, 128 devices: a whole 4x4x4 slice. The times are simulated.
128 devices in a mesh: vp: 128 (over z, y, x, core).
Axes of the slice: x: 4, y: 4, z: 4, core: 2. Of those that a mesh axis runs over, the one named last changes fastest.
Arguments:
- residual: bfloat16 [16384, 2048], replicated
- labels: int32 [16384], replicated
- loss_mask: float32 [16384], replicated
- norm_gain: float32 [2048], replicated
- embed_table: bfloat16 [49408, 2048], P('vp')
Outputs:
- output 1: float32 [], replicated
- output 2: float32 [16384, 2048], P('vp')
- output 3: float32 [49408, 2048], P('vp')
- output 4: float32 [2048], replicated
All inputs are finite; a program needn't handle non-finite values.
Results may differ from a plain program's by a relative error of at most 0.001.
Values sent between devices are 32-bit elements.
A program may use at most 1 GiB of HBM per device.

v0:
```python
import functools
import itertools
import math

import jax
import jax.numpy as jnp
from jax import lax
from jax.experimental import pallas as pl
from jax.experimental.pallas import tpu as pltpu
from jax.sharding import PartitionSpec as P

VOCAB_REAL = 49155
LOGIT_SCALE = 6.0
NORM_EPS = 1e-6

AXIS = "vp"
MESH = pl.DeviceIdType.MESH
F32 = jnp.float32
BF16 = jnp.bfloat16
HBM = pltpu.HBM
VMEM = pltpu.VMEM
DMA = pltpu.SemaphoreType.DMA


def _coords():
    me = lax.axis_index(AXIS)
    return me // 32, (me // 8) % 4, (me // 2) % 4, me % 2


def _dev(z, y, x, c):
    return ((z * 4 + y) * 4 + x) * 2 + c


def _mod4(v):
    return lax.rem(v + 8, 4)


def _barrier(peers):
    sem = pltpu.get_barrier_semaphore()
    for p in peers:
        pl.semaphore_signal(sem, inc=1, device_id=(p,), device_id_type=MESH)
    pl.semaphore_wait(sem, len(peers))


def _remote(src, dst, send, recv, k, dev):
    return pltpu.make_async_remote_copy(
        src_ref=src,
        dst_ref=dst,
        send_sem=send.at[k],
        recv_sem=recv.at[k],
        device_id=(dev,),
        device_id_type=MESH,
    )


LANES = 128


class Dims:
    def __init__(self, tokens, dim, rows, group):
        self.dim, self.rows = dim, rows
        unit = LANES if rows >= LANES else 64
        self.rm = rows // unit * unit
        self.ha = self.rm // 2
        low = max(16, self.ha // 48 * 16)
        self.cuts = ((low, self.ha - low), (0, low))
        self.pad = self.rm + 8
        self.chunk = tokens // group
        self.tok = 16 * self.chunk
        self.nt = 4 * self.chunk
        self.main = 8 * self.rm
        self.wide = self.main + LANES
        self.h = dim // 2


def _top(n):
    return pl.ds(0, n)


def _rem(a, b):
    return a % b if isinstance(a, int) else lax.rem(a, b)


def _pick(test, a, b):
    return (a if test else b) if isinstance(test, bool) else jnp.where(test, a, b)


def _loop_rows(rows, step, fn):
    @pl.loop(0, rows // step)
    def _(i):
        fn(pl.ds(pl.multiple_of(i * step, step), step))


def _add_rows(dst, srcs, step):
    def add(r):
        acc = dst[r, :]
        for s in srcs:
            acc = acc + s[r, :]
        dst[r, :] = acc

    _loop_rows(dst.shape[0], step, add)


SLOTS = 12
FEW = 64
TWO = range(2)
LOG2E = math.log2(math.e)
NEAR_KEYS = ("near_r", "near_l", "sum_r", "sum_l")
scope = jax.named_scope


def _kernel(
    dm, x4, e_ref, g_ref, lab, msk,
    dx_out, got2, q_o, xs, xe, eg, zh, q_h, xa, xb, dhp, yr,
    hv, etv, dz, od, sst, few, oext, ya, yb, yl, za, zb, zl, zr, tst,
    m_row, s_row, w_row, pos_row, lse_row, tgt_row, got, sm, got1, total_v,
    send, recv,
    free, tsem, hsem, dsem, osem, lsem,
):
    z, y, x, c = _coords()
    xc, zy = x * 2 + c, z * 4 + y
    rows, rm, ha, dim, h = dm.rows, dm.rm, dm.ha, dm.dim, dm.h
    chunk, tok, nt, hc = dm.chunk, dm.tok, dm.nt, dm.h // 2
    x_far, x_p, x_m = _mod4(x + 2), _mod4(x + 1), _mod4(x - 1)
    xp, xm = _dev(z, y, x_p, c), _dev(z, y, x_m, c)
    yp, ym = _dev(z, _mod4(y + 1), x, c), _dev(z, _mod4(y - 1), x, c)
    zp, zm = _dev(_mod4(z + 1), y, x, c), _dev(_mod4(z - 1), y, x, c)
    sib = _dev(z, y, x, 1 - c)
    near = [_dev(_mod4(z + a), _mod4(y + b), x, c) for a in range(4) for b in range(4) if a or b]
    line = [_dev(z, y, _mod4(x + a), lax.rem(c + b, 2)) for a in range(4) for b in TWO if a or b]
    bar = pltpu.get_barrier_semaphore()
    for p in (*near, *line):
        pl.semaphore_signal(bar, inc=1, device_id=(p,), device_id_type=MESH)
    sent = []
    ids = itertools.count()

    def remote(src, dst, dev):
        cp = _remote(src, dst, send, recv, next(ids), dev)
        cp.start()
        sent.append(cp)
        return cp

    def exchange(src, dst, devs):
        k = next(ids)
        for i, dev in enumerate(devs):
            _remote(src, dst.at[i], send, recv, k, dev).start()
        whole = dst.at[_top(len(devs))]
        return pltpu.make_async_copy(whole, whole, recv.at[k]), pltpu.make_async_copy(whole, whole, send.at[k])

    def local(src, dst, sem):
        cp = pltpu.make_async_copy(src, dst, sem)
        cp.start()
        return cp

    x_at, ext_at = 2 * rm, 4 * rm

    def xload(k):
        s = lax.rem(k, 4)
        to = dz.at[pl.ds(pl.multiple_of(x_at + s * chunk, chunk), chunk)]
        return pltpu.make_async_copy(x4.at[k, xc], to, tsem.at[s])

    with scope("prep"):
        for k in range(3):
            xload(k).start()
        own = xc
        cps = []
        for j in TWO:
            def widen(r, j=j):
                od[0, j, r, :] = e_ref[pl.ds(j * ha + r.start, r.size), :].astype(F32)

            _loop_rows(ha, 16, widen)
            cps.append(local(od.at[0, j, _top(ha)], eg.at[own, pl.ds(j * ha, ha)], hsem.at[j]))
        oext[...] = jnp.zeros_like(oext)
        oext[0 : rows - rm, :] = e_ref[rm:rows, :].astype(F32)
        cps.append(local(oext, eg.at[own, pl.ds(rm, 8)], hsem.at[2]))
        pl.semaphore_wait(bar, 22)

    half_a, half_b = _top(ha), pl.ds(ha, ha + 8)
    cut = ha + 8
    part_r, part_l, strip = _top(cut), pl.ds(cut, dm.pad - cut), pl.ds(ha, cut - ha)

    def piece(s, r, dev):
        return remote(eg.at[s, r], eg.at[s, r], dev)

    def slot(xx):
        return xx * 2 + c

    cps[0].wait()
    r_a = piece(own, half_a, xp)
    for cp in cps[1:]:
        cp.wait()
    l_b = piece(own, half_b, xm)
    s_o = piece(own, _top(dm.pad), sib)
    r_b, l_a = piece(own, half_b, xp), piece(own, half_a, xm)

    gain = g_ref[...]

    with scope("norm"):
        @pl.loop(0, 16)
        def _(k):
            @pl.when(k < 13)
            def _():
                xload(k + 3).start()

            xload(k).wait()

            def norm(r):
                v = dz[pl.ds(pl.multiple_of(x_at + lax.rem(k, 4) * chunk + r.start, r.size), r.size), :].astype(F32)
                inv = lax.rsqrt(jnp.mean(v * v, axis=-1, keepdims=True) + NORM_EPS)
                hv[pl.ds(pl.multiple_of(k * chunk + r.start, r.size), r.size), :] = (v * inv * gain).astype(BF16)

            _loop_rows(chunk, 16, norm)

    with scope("labels"):
        total = jnp.sum(msk[...])
        for k in range(16):
            at = pl.ds(k * chunk, chunk)
            w_row[:, at] = msk[k, xc] / total
            q = lab[k, xc] - zy * (8 * rows)
            s = jnp.zeros_like(q)
            for i in range(1, 8):
                s = s + jnp.where(q >= i * rows, 1, 0)
            r = q - s * rows
            up = jnp.where(r >= ha, 1, 0)
            at_main = ((s // 2 * 2 + up) * 2 + s % 2) * ha + r - up * ha
            at_ext = dm.main + s * 8 + r - rm
            place = jnp.where(r < rm, at_main, at_ext)
            pos_row[:, at] = jnp.where((q >= 0) & (q < 8 * rows), place, -1).astype(F32)

    def product(lhs, lanes):
        v = lax.dot_general(lhs, hv[lanes, :], (((1,), (1,)), ((), ())), preferred_element_type=F32)
        return v * (LOG2E / LOGIT_SCALE)

    def add_stats(v, lanes):
        m_old, s_old = m_row[:, lanes], s_row[:, lanes]
        m = jnp.maximum(m_old, jnp.max(v, axis=0, keepdims=True))
        s = jnp.sum(jnp.exp2(v - m), axis=0, keepdims=True)
        m_row[:, lanes] = m
        s_row[:, lanes] = s_old * jnp.exp2(m_old - m) + s

    def add_target(v, place, lanes):
        r = lax.broadcasted_iota(jnp.int32, v.shape, 0)
        hit = r.astype(F32) == pos_row[:, lanes] - place.astype(F32)
        tgt_row[:, lanes] += jnp.sum(jnp.where(hit, v, 0.0), axis=0, keepdims=True)

    m_row[:, :] = jnp.full((1, tok), -jnp.inf, F32)
    s_row[:, :] = jnp.zeros((1, tok), F32)
    tgt_row[:, :] = jnp.zeros((1, tok), F32)
    segs = [(half, j) for half in TWO for j in TWO]

    def load(r0, n, xx, cores=TWO):
        return [
            local(
                eg.at[xx[half] * 2 + j, pl.ds(half * ha + r0, n)],
                od.at[j, half, pl.ds(r0, n)],
                hsem.at[half * len(cores) + k],
            )
            for half in TWO
            for k, j in enumerate(cores)
        ]

    def narrow_all(r0, n, src, cores=TWO):
        for half in TWO:
            for j in cores:
                def narrow(r, half=half, j=j):
                    at = pl.multiple_of((half * 2 + j) * ha + r0 + r.start, r.size)
                    dz[pl.ds(at, r.size), :] = src(half, j)[r, :].astype(BF16)

                _loop_rows(n, 16, narrow)

    def load_narrow(r0, n, xx, core):
        for cp in load(r0, n, xx, (core,)):
            cp.wait()
        narrow_all(r0, n, lambda half, j: od.at[j, half, pl.ds(r0, n)], (core,))

    def block(r0, n, xx, loads=(), with_few=False, nt=nt):
        if loads:
            for cp in loads:
                cp.wait()
            narrow_all(r0, n, lambda half, j: od.at[j, half, pl.ds(r0, n)])
        left = [VOCAB_REAL - ((zy * 8 + xx[half] * 2 + j) * rows + half * ha + r0) for half, j in segs]
        w, tall = nt // chunk, len(segs) * n
        pack = tst.shape[1] // tall
        deep = SLOTS // w
        packed = SLOTS * pack >= tok // chunk

        def place(t, i):
            if packed:
                return t * (w // pack) + i // pack, i % pack * tall
            return lax.rem(t, deep) * w + i, 0

        def out(t):
            cps = []
            for i in range(w):
                u, row = place(t, i)
                for m, (half, j) in enumerate(segs):
                    to = pl.ds(pl.multiple_of((xx[half] * 2 + half) * rm + j * ha + r0, 8), n)
                    cps.append(pltpu.make_async_copy(tst.at[u, pl.ds(row + m * n, n)], zh.at[t * w + i, to], tsem.at[u]))
            return cps

        def out_wait(u, rows_):
            whole = tst.at[u, _top(rows_)]
            pltpu.make_async_copy(whole, whole, tsem.at[u]).wait()

        @pl.loop(0, tok // nt)
        def _(t):
            if not packed:
                @pl.when(t >= deep)
                def _():
                    for i in range(w):
                        out_wait(place(t, i)[0], tall)

            lanes = pl.ds(pl.multiple_of(t * nt, nt), nt)
            lhs = [dz[(half * 2 + j) * ha + r0 : (half * 2 + j) * ha + r0 + n, :] for half, j in segs]
            if with_few:
                lhs.append(dz[ext_at : ext_at + FEW, :])
            v = product(jnp.concatenate(lhs, axis=0), lanes)
            v, v_few = v[:tall], v[tall:]
            r = lax.broadcasted_iota(jnp.int32, (n, nt), 0)
            v = [jnp.where(r < left[m], v[m * n : (m + 1) * n], -jnp.inf) for m in range(len(segs))]
            for part_v, (half, j) in zip(v, segs):
                add_target(part_v, (xx[half] * 2 + half) * rm + j * ha + r0, lanes)
            for i in range(w):
                u, row = place(t, i)
                for m in range(len(segs)):
                    tst[u, row + m * n : row + (m + 1) * n, :] = v[m][:, i * chunk : (i + 1) * chunk]
            if with_few:
                r = lax.broadcasted_iota(jnp.int32, v_few.shape, 0)
                ok = ((r & 7) < rows - rm) & ((zy * 8 + (r >> 3)) * rows + rm + (r & 7) < VOCAB_REAL)
                v_few = jnp.where(ok, v_few, -jnp.inf)
                few[:, lanes] = v_few
                add_target(v_few, jnp.int32(dm.main), lanes)
                v.append(v_few)
            v = jnp.concatenate(v, axis=0)
            for cp in out(t):
                cp.start()
            add_stats(v, lanes)

        if packed:
            for u in range(tok // chunk // pack):
                out_wait(u, pack * tall)
        else:
            for u in range(deep * w):
                out_wait(u, tall)

    def both(xx):
        block(0, ha, xx, load(0, ha, xx))

    def turn(xx):
        for half in TWO:
            base = pl.multiple_of((xx[half] * 2 + half) * rm, rm)

            @pl.loop(0, dim // LANES)
            def _(d, half=half, base=base):
                at = pl.ds(pl.multiple_of(d * LANES, LANES), LANES)
                etv[at, pl.ds(base, rm)] = dz[half * rm : (half + 1) * rm, at].T

    with scope("own"):
        s_o.wait_recv()
        both((x, x))
        turn((x, x))

    with scope("wait_1"):
        r_a.wait_recv()
        last_n = dm.cuts[-1][1]
        spans = [(pl.ds(r0, n), pl.ds(ha + r0, n + 8 * (r0 + n == ha))) for r0, n in dm.cuts]

        def far_pieces(xx, half, to):
            cps = [piece(slot(xx), pair[half], to) for pair in spans[:-1]]
            cps.append(remote(eg.at[slot(xx), spans[-1][half]], sst.at[c, pl.ds(half * last_n, last_n)], to))
            return cps

        r_f = far_pieces(x_m, 0, xp)
        d = [piece(slot(x_m), half_a, sib)]
        l_b.wait_recv()
        l_f = far_pieces(x_p, 1, xm)
        d.append(piece(slot(x_p), half_b, sib))
        for cp in d:
            cp.wait_recv()

    with scope("near_1"):
        both((x_m, x_p))
        turn((x_m, x_p))

    with scope("wait_2"):
        r_b.wait_recv()
        d = [piece(slot(x_m), half_b, sib)]
        l_a.wait_recv()
        d.append(piece(slot(x_p), half_a, sib))
        for cp in d:
            cp.wait_recv()

    with scope("near_2"):
        both((x_p, x_m))
        turn((x_p, x_m))

    far = (x_far, x_far)

    with scope("wait_3"):
        d = []
        for cp, r in zip((r_f[0], l_f[0]), spans[0]):
            cp.wait_recv()
            d.append(piece(slot(x_far), r, sib))
        load_narrow(*dm.cuts[0], far, c)
        for cp in d:
            cp.wait_recv()
    with scope("far_a"):
        ext_loads = [local(eg.at[s, pl.ds(rm, 8)], few.at[pl.ds(s * 8, 8)], lsem.at[s]) for s in range(8)]
        load_narrow(*dm.cuts[0], far, 1 - c)
        for cp in ext_loads:
            cp.wait()
        dz[ext_at : ext_at + FEW, :] = few[...].astype(BF16)
        dz[ext_at + FEW : ext_at + LANES, :] = jnp.zeros((FEW, dim), BF16)
        block(*dm.cuts[0], far, with_few=True)
    with scope("wait_5"):
        over = []
        for half, cp in enumerate((r_f[-1], l_f[-1])):
            cp.wait_recv()
            ref = sst.at[c, pl.ds(half * last_n, last_n)]
            over.append(_remote(ref, ref, send, recv, next(ids), sib))
            over[-1].start()

        @pl.loop(0, dim // LANES)
        def _(i):
            at = pl.ds(pl.multiple_of(i * LANES, LANES), LANES)
            etv[at, dm.main : dm.wide] = dz[ext_at : ext_at + LANES, at].T

        def last_rows(half, j):
            return sst.at[j, pl.ds(half * last_n, last_n)]

        narrow_all(0, last_n, last_rows, (c,))
        for cp in over:
            cp.wait_recv()

    with scope("far_c"):
        narrow_all(0, last_n, last_rows, (1 - c,))
        block(0, last_n, far, nt=8 * chunk)
        for cp in over:
            cp.wait_send()
        for s in TWO:
            pl.semaphore_signal(free.at[s], inc=1, device_id=(sib,), device_id_type=MESH)

    with scope("turn_far"):
        lse_row[:, :] = m_row[:, :] + jnp.log(s_row[:, :]) * LOG2E
        stats = exchange(lse_row, got, near)
        turn(far)

    wide = 2 * rm

    at_dht = SLOTS - 4

    def chunk_of(zz, yy):
        return _mod4(zz) * 4 + _rem(yy + 8, 4)

    def all_far(i):
        return x_far * wide + i // 16 * rm, _rem(i, 16)

    def in_order(i):
        n = i // 3
        m = n - 7
        k = _pick(n < 7, chunk_of(z + n - 1, y + 2), chunk_of(z + 3 + m // 3, y + 3 + _rem(m + 9, 3)))
        return _mod4(x + 3 + _rem(i, 3)) * wide, _pick(n < 4, chunk_of(z + 2, n), k)

    def later(i):
        return in_order(i + SLOTS)

    def zload(where, i, ring, n):
        at, k = where(i)
        s = _rem(i, ring)
        src = zh.at[k, pl.ds(pl.multiple_of(at, rm), n)]
        return pltpu.make_async_copy(src, tst.at[s, _top(n)], tsem.at[s])

    def zahead(where, ring, n):
        for i in range(ring):
            zload(where, i, ring, n).start()

    with scope("stats"):
        zahead(all_far, SLOTS, rm)
        for cp in stats:
            cp.wait()
        top = lse_row[:, :]
        for k in range(len(near)):
            top = jnp.maximum(top, got[k])
        s = jnp.exp2(lse_row[:, :] - top)
        for k in range(len(near)):
            s = s + jnp.exp2(got[k] - top)
        lse_row[:, :] = top + jnp.log(s) * LOG2E

    def dz_part(v, place, at, lanes):
        r = lax.broadcasted_iota(jnp.int32, v.shape, 0).astype(F32)
        hit = r == pos_row[:, lanes] - place.astype(F32)
        p = jnp.exp2(v - lse_row[:, lanes])
        dz[at, lanes] = (jnp.where(hit, p - 1.0, p) * w_row[:, lanes]).astype(BF16)

    step = min(LANES, rm)

    def dz_rows(where, start, stop, last_tile, ring, n):
        @pl.loop(start, stop)
        def _(i):
            @pl.when((i > 0) & (i + ring - 1 < last_tile))
            def _():
                zload(where, i + ring - 1, ring, n).start()

            zload(where, i, ring, n).wait()
            row, k = where(i)
            lanes = pl.ds(pl.multiple_of(k * chunk, chunk), chunk)

            @pl.loop(0, n // step)
            def _(j):
                at = pl.multiple_of(row + j * step, step)
                r = pl.ds(pl.multiple_of(j * step, step), step)
                dz_part(tst[lax.rem(i, ring), r, :], at, pl.ds(at, step), lanes)

    def dz_far(start, stop):
        dz_rows(all_far, start, stop, 32, SLOTS, rm)

    with scope("dz_far"):
        dz_far(0, 16)

    nd = dim // 2
    few_rows = pl.ds(dm.main, FEW)
    pair_ids = [(next(ids), next(ids)) for _ in TWO]

    def over_d2d(s, n, i):
        lanes = pl.ds(pl.multiple_of(i * nd, nd), nd)
        there = sst.at[s, _top(n), lanes]
        return _remote(od.at[s, 1 - c, _top(n), lanes], there, send, recv, pair_ids[s][0] + i, sib)

    def de_block(xx, half, s, with_few=False):
        at = pl.ds(pl.multiple_of((xx * 2 + half) * rm, rm), rm)
        n = ha + 8 * half
        pl.semaphore_wait(free.at[s], 1)

        @pl.loop(0, 2)
        def _(i):
            lanes = pl.ds(pl.multiple_of(i * nd, nd), nd)
            lhs = jnp.concatenate([dz[at, :], dz[few_rows, :]], axis=0) if with_few else dz[at, :]
            v = jnp.dot(lhs, hv[:, lanes], preferred_element_type=F32)
            if with_few:
                few[:, lanes] = v[rm:]
            for j in TWO:
                od[s, j, 0:ha, lanes] = v[j * ha : (j + 1) * ha]
                if half:
                    od[s, j, ha:n, lanes] = few[pl.ds(pl.multiple_of((xx * 2 + j) * 8, 8), 8), lanes]
            over_d2d(s, n, i).start()

        return half, s, n

    def stored(blk, to):
        half, s, n = blk
        return pltpu.make_async_copy(od.at[s, c, _top(n)], to.at[pl.ds(half * ha, n)], dsem.at[s])

    def early(blk, src):
        half, s, n = blk
        for i in TWO:
            over_d2d(s, n, i).wait_send()
        return local(src.at[pl.ds(half * ha, n)], od.at[s, 1 - c, _top(n)], lsem.at[s])

    def sum_add(blk, to, more=None):
        half, s, n = blk
        for i in TWO:
            over_d2d(s, n, i).wait_recv()
        if more is not None:
            more.wait()

        def add(r):
            v = od[s, c, r, :] + sst[s, r, :]
            od[s, c, r, :] = v if more is None else v + od[s, 1 - c, r, :]

        _loop_rows(n, 8, add)
        if more is None:
            pl.semaphore_signal(free.at[s], inc=1, device_id=(sib,), device_id_type=MESH)
            for i in TWO:
                over_d2d(s, n, i).wait_send()
        cp = stored(blk, to)
        cp.start()
        return cp

    def ring_sum(xx, rows_, n, src, s, dst, dev):
        lds = [
            local(q_h.at[xx, rows_], od.at[s, 0, _top(n)], lsem.at[0]),
            local(src, od.at[s, 1, _top(n)], lsem.at[1]),
        ]
        for cp in lds:
            cp.wait()
        _add_rows(od.at[s, 0, _top(n)], [od.at[s, 1, _top(n)]], 8)
        local(od.at[s, 0, _top(n)], q_h.at[xx, rows_], lsem.at[0]).wait()
        return remote(q_h.at[xx, rows_], dst, dev)

    stores = []

    def flush():
        while stores:
            stores.pop().wait()

    def tiles(q, where, between=None):
        flush()

        def outs(i):
            p, ab = where(i)
            r = pl.ds(q * h, h)
            dsts = [dhp.at[ab * 2 + j, p, r] if q == 0 else dhp.at[p, ab * 2 + j, r] for j in TWO]
            return [
                pltpu.make_async_copy(tst.at[at_dht + i * 2 + j, _top(h)], dst, hsem.at[i * 2 + j])
                for j, dst in enumerate(dsts)
            ]

        @pl.loop(0, 2)
        def _(i):
            if between is not None:
                pl.when(i > 0)(between)
            p, ab = where(i)
            ks = [(ab * 2 + j) * 4 + p if q == 0 else p * 4 + ab * 2 + j for j in TWO]
            rhs = jnp.concatenate([dz[:, pl.ds(pl.multiple_of(k * chunk, chunk), chunk)] for k in ks], axis=1)
            v = jnp.dot(etv[q * h : (q + 1) * h, :], rhs, preferred_element_type=F32)
            for j in TWO:
                tst[at_dht + i * 2 + j, 0:h, :] = v[:, j * chunk : (j + 1) * chunk]
            for cp in outs(i):
                cp.start()

        for i in TWO:
            stores.extend(outs(i))

    def part(q, p, lo, n):
        r = pl.ds(q * h, h)
        if q == 0:
            return dhp.at[pl.ds(lo, n), p, r]
        return dhp.at[p, pl.ds(lo, n), r]

    def one(q, p, i):
        r = pl.ds(q * h, h)
        return dhp.at[i, p, r] if q == 0 else dhp.at[p, i, r]

    ring1, ring2 = ((yp, ym), (zp, zm)), ((zp, zm), (yp, ym))
    pos1, pos2 = (y, z), (z, y)
    first, second = ({}, {}), ({}, {})

    def send_far(q):
        flush()
        p, (rt, lt) = pos1[q], ring1[q]
        first[q]["far_r"] = remote(part(q, _mod4(p + 2), 0, 2), ya.at[q], rt)
        first[q]["far_l"] = remote(part(q, _mod4(p + 2), 2, 2), yb.at[q], lt)

    def send_near(q):
        flush()
        p, (rt, lt) = pos1[q], ring1[q]
        first[q]["near_r"] = remote(part(q, _mod4(p + 1), 2, 2), yl.at[q, pl.ds(2, 2)], rt)
        first[q]["near_l"] = remote(part(q, _mod4(p - 1), 0, 2), yr.at[q, _top(2)], lt)

    def fetch(i, src):
        return local(src, tst.at[i, _top(h)], tsem.at[i])

    def pass_on(q):
        flush()
        p, (rt, lt) = pos1[q], ring1[q]
        lds = [fetch(i, one(q, _mod4(p + 1), i)) for i in TWO]
        lds += [fetch(2 + i, one(q, _mod4(p - 1), 2 + i)) for i in TWO]
        first[q]["far_r"].wait_recv()
        for i in TWO:
            lds[i].wait()
            _add_rows(ya.at[q, i], [tst.at[i, _top(h)]], min(FEW, h))
        first[q]["sum_r"] = remote(ya.at[q], yl.at[q, _top(2)], rt)
        first[q]["far_l"].wait_recv()
        for i in TWO:
            lds[2 + i].wait()
            _add_rows(yb.at[q, i], [tst.at[2 + i, _top(h)]], min(FEW, h))
        first[q]["sum_l"] = remote(yb.at[q], yr.at[q, pl.ds(2, 2)], lt)

    lo, hi = _top(hc), pl.ds(hc, hc)

    def second_phase(q):
        flush()
        r, (rt, lt) = pos2[q], ring2[q]
        r2, r1, rm1 = _mod4(r + 2), _mod4(r + 1), _mod4(r - 1)
        order = (r2, r1, rm1, r)
        lds = [fetch(i, one(q, pos1[q], k)) for i, k in enumerate(order)]
        for k in NEAR_KEYS:
            first[q][k].wait_recv()
        lds2 = [fetch(4 + i, yr.at[q, k]) for i, k in enumerate(order)]
        for i, k in enumerate(order):
            lds[i].wait()
            lds2[i].wait()
            _add_rows(yl.at[q, k], [tst.at[i, _top(h)], tst.at[4 + i, _top(h)]], min(FEW, h))
            if i == 0:
                second[q]["far_r"] = remote(yl.at[q, r2, lo], za.at[q], rt)
                second[q]["far_l"] = remote(yl.at[q, r2, hi], zb.at[q], lt)
            if i == 1:
                second[q]["near_r"] = remote(yl.at[q, r1, hi], zl.at[q, hi], rt)
            if i == 2:
                second[q]["near_l"] = remote(yl.at[q, rm1, lo], zr.at[q, lo], lt)

    def second_pass(q):
        r, (rt, lt) = pos2[q], ring2[q]
        r1, rm1 = _mod4(r + 1), _mod4(r - 1)
        second[q]["far_r"].wait_recv()
        _add_rows(yl.at[q, r1, lo], [za.at[q]], min(FEW, hc))
        second[q]["sum_r"] = remote(yl.at[q, r1, lo], zl.at[q, lo], rt)
        second[q]["far_l"].wait_recv()
        _add_rows(yl.at[q, rm1, hi], [zb.at[q]], min(FEW, hc))
        second[q]["sum_l"] = remote(yl.at[q, rm1, hi], zr.at[q, hi], lt)

    def last(q):
        r = pos2[q]
        for k in NEAR_KEYS:
            second[q][k].wait_recv()
        n = min(LANES, h)

        @pl.loop(0, h // n)
        def _(i):
            at = pl.ds(pl.multiple_of(i * n, n), n)
            v = yl[q, r, at, :] + zl[q, at, :] + zr[q, at, :]
            od[0, 0, 0:chunk, pl.ds(pl.multiple_of(q * h + i * n, n), n)] = (v * (1.0 / LOGIT_SCALE)).T

    def tiles_far(q, between=None):
        tiles(q, lambda i: (_mod4(pos1[q] + 2), i), between)

    def tiles_near(q):
        tiles(q, lambda i: (_mod4(pos1[q] + 1 + 2 * i), 1 - i))

    def tiles_pass(q):
        tiles(q, lambda i: (_mod4(pos1[q] + 1 + 2 * i), i))

    def tiles_own(q):
        tiles(q, lambda i: (pos1[q], i))

    all_later = 48 - SLOTS

    def dz_first(start, stop):
        dz_rows(in_order, start, stop, SLOTS, SLOTS, wide)

    def dz_later(start, stop):
        dz_rows(later, start, stop, all_later, at_dht, wide)

    with scope("de_far"):
        b0 = de_block(x_far, 0, 0)
        dz_far(16, 32)
        zahead(in_order, SLOTS, wide)
        for l in range(0, tok, nt):
            lanes = pl.ds(l, nt)
            dz_part(few[:, lanes], jnp.int32(dm.main), few_rows, lanes)
        dz[dm.main + FEW : dm.wide, :] = jnp.zeros((FEW, tok), BF16)
        b1 = de_block(x_far, 1, 1, True)
    with scope("dz_1"):
        c0 = sum_add(b0, q_h.at[x_far])
        dz_first(0, 8)
        c0.wait()
        e0 = [remote(q_h.at[x_far, half_a], xa.at[half_a], xp)]
        dz_first(8, SLOTS)
        zahead(later, at_dht, wide)
    with scope("dh_far1"):
        def between():
            sum_add(b1, q_h.at[x_far])

        tiles_far(1, between)
        c1 = stored(b1, q_h.at[x_far])
        c1.wait()
        e1 = remote(q_h.at[x_far, part_l], xb, xm)
        e0.append(remote(q_h.at[x_far, strip], xa.at[strip], xp))
    with scope("dz_2"):
        dz_later(0, 9)
        send_far(1)
    with scope("dh_far0"):
        tiles_far(0)
    with scope("dz_3"):
        dz_later(9, 13)
        send_far(0)
        dz_later(13, all_later)
    with scope("de_2"):
        b2 = de_block(x_p, 1, 0)
        b3 = de_block(x_m, 0, 1)
        c2 = sum_add(b2, q_h.at[x_p])
    with scope("dh_near"):
        tiles_near(1)
        c2.wait()
        e2 = remote(q_h.at[x_p, part_l], xe.at[part_l], xp)
        c3 = sum_add(b3, q_h.at[x_m])
        send_near(1)
        tiles_near(0)
        c3.wait()
        e3 = [remote(q_h.at[x_m, half_a], xe.at[half_a], xm)]
        send_near(0)
    with scope("dh_pass"):
        tiles_pass(1)
        tiles_pass(0)
        pass_on(1)
    with scope("de_4"):
        b4 = de_block(x_p, 0, 0)
        pass_on(0)
        b5 = de_block(x_m, 1, 1)
        c4 = sum_add(b4, q_h.at[x_p])
    with scope("dh_own"):
        tiles_own(1)
        c5 = sum_add(b5, q_h.at[x_m])
        tiles_own(0)
        c4.wait()
        c5.wait()
        e3.append(remote(q_h.at[x_m, strip], xe.at[strip], xm))
    old = list(sent)
    sent.clear()
    with scope("ring"):
        for cp in e0:
            cp.wait_recv()
        e4 = ring_sum(x_p, part_r, cut, xa, 0, xs.at[part_r], xp)
        e1.wait_recv()
        e5 = ring_sum(x_m, part_l, dm.pad - cut, xb, 1, xs.at[part_l], xm)
    with scope("de_6"):
        b6 = de_block(x, 0, 0)
    with scope("de_7"):
        b7 = de_block(x, 1, 1)
        xo_load = local(x4.at[zy, xc], dz.at[_top(chunk)], osem.at[0])
    with scope("second_1"):
        second_phase(1)
    with scope("second_0"):
        second_phase(0)
    with scope("spass_1"):
        second_pass(1)
    with scope("sum_6"):
        for cp in e3:
            cp.wait_recv()
        c6 = early(b6, xe)
        e2.wait_recv()
        c7 = early(b7, xe)
        c6 = sum_add(b6, q_o, c6)
        c7 = sum_add(b7, q_o, c7)
    with scope("spass_0"):
        second_pass(0)
        c6.wait()
        c7.wait()
    def drain(cps):
        while cps:
            cps.pop().wait_send()

    def own_x(r):
        v = dz[r, :].astype(F32)
        inv = lax.rsqrt(jnp.mean(v * v, axis=-1, keepdims=True) + NORM_EPS)
        od[1, 0, r, :] = v * inv
        od[1, 1, r, 0:LANES] = jnp.broadcast_to(inv, (r.size, LANES))

    def own_dg(q):
        lanes = pl.ds(q * h, h)

        def add(i, acc):
            r = pl.ds(pl.multiple_of(i * 8, 8), 8)
            return acc + od[0, 0, r, lanes] * od[1, 0, r, lanes]

        acc = lax.fori_loop(0, chunk // 8, add, jnp.zeros((8, h), F32))
        sm[:, lanes] = jnp.sum(acc, axis=0, keepdims=True)

    def own_dx(r):
        x_hat, u = od[1, 0, r, :], od[0, 0, r, :] * gain
        od[0, 1, r, :] = od[1, 1, r, 0:1] * (u - x_hat * jnp.mean(u * x_hat, axis=-1, keepdims=True))

    with scope("own_x"):
        xo_load.wait()
        _loop_rows(chunk, 16, own_x)
        lse = jnp.where(zy == 0, lse_row[:, :], 0.0)
        loss = jnp.sum(w_row[:, :] * (lse - tgt_row[:, :]))
        sm[:, dim : dim + LANES] = jnp.full((1, LANES), loss / LOG2E)
        drain(old)
    with scope("last_1"):
        last(1)
        own_dg(1)
    with scope("last_0"):
        last(0)
        own_dg(0)

    with scope("small_1"):
        old = [cp for cp in sent if cp is not e4 and cp is not e5]
        near_sums = exchange(sm, got1, near)
        _loop_rows(chunk, 16, own_dx)
        dx_copy = local(od.at[0, 1, _top(chunk)], dx_out, osem.at[0])
        drain(old)
        for cp in near_sums:
            cp.wait()
    with scope("small_2"):
        tot = sm[...]
        for k in range(len(near)):
            tot = tot + got1[k]
        total_v[...] = tot
        all_sums = exchange(total_v, got2, line)
        mine = local(total_v, got2.at[len(line)], osem.at[1])
    with scope("ring_end"):
        for cp in (e4, e5):
            cp.wait()
        dx_copy.wait()
        mine.wait()
    with scope("small_3"):
        for cp in all_sums:
            cp.wait()


def _run(dm, x4, table, gain, labels, mask):
    hbm, vm = pl.BlockSpec(memory_space=HBM), pl.BlockSpec(memory_space=VMEM)
    sd = jax.ShapeDtypeStruct
    d, tok, h, ck, pad, ha = dm.dim, dm.tok, dm.h, dm.chunk, dm.pad, dm.ha
    line, quad, pair = VMEM((1, tok), F32), VMEM((2, 2, h, ck), F32), VMEM((2, h, ck), F32)
    part, shard = VMEM((2, h // 2, ck), F32), sd((pad, d), F32)
    out = pl.pallas_call(
        functools.partial(_kernel, dm),
        name="head",
        out_shape=(
            sd((ck, d), F32), sd((8, 1, d + LANES), F32),
            shard, shard, shard,
            sd((8, pad, d), F32), sd((16, dm.main, ck), F32),
            sd((4, pad, d), F32), sd((ha + 8, d), F32), sd((ha, d), F32),
            sd((4, 4, d, ck), F32), sd((2, 4, h, ck), F32),
        ),
        in_specs=[hbm, vm, vm, vm, vm],
        out_specs=[hbm] * 12,
        scratch_shapes=[
            VMEM((tok, d), BF16), VMEM((d, dm.wide), BF16), VMEM((dm.wide, tok), BF16),
            VMEM((2, 2, ha + 8, d), F32), VMEM((2, ha + 8, d), F32), VMEM((FEW, d), F32), VMEM((8, d), F32),
            quad, quad, VMEM((2, 4, h, ck), F32),
            part, part, pair, pair,
            VMEM((SLOTS, max(h, 2 * dm.rm), ck), F32),
            line, line, line, line, line, line, VMEM((15, 1, tok), F32),
            VMEM((1, d + LANES), F32), VMEM((15, 1, d + LANES), F32), VMEM((1, d + LANES), F32),
            DMA((56,)), DMA((56,)), pltpu.SemaphoreType.REGULAR((2,)),
            DMA((SLOTS,)), DMA((4,)), DMA((2,)), DMA((2,)), DMA((8,)),
        ],
        compiler_params=pltpu.CompilerParams(
            collective_id=0, has_side_effects=True, vmem_limit_bytes=67043328
        ),
    )(x4, table, gain, labels, mask)
    return _write_out(dm, out[2:4], *out[:2])


def _write_kernel(own, ring, dx, small, de_o, dx_o, dg_o, loss_o):
    de_o[:, :] = (own[:, :] + ring[:, :]) * (1.0 / LOGIT_SCALE)
    dx_o[:, :] = dx[:, :]
    total = jnp.sum(small[:, :, :], axis=0)
    d = dg_o.shape[1]
    dg_o[:, :] = total[:, :d]
    loss_o[:, :] = total[:, d : d + 1]


def _write_out(dm, parts, dx, small):
    d, step, blocks = dm.dim, dm.ha + 8, 2
    sd = jax.ShapeDtypeStruct
    some = pl.BlockSpec((step, d), lambda i: (i, 0))
    half = pl.BlockSpec((dm.chunk // blocks, d), lambda i: (i, 0))
    row, one = pl.BlockSpec((1, d), lambda i: (0, 0)), pl.BlockSpec((1, 1), lambda i: (0, 0))
    rows = pl.BlockSpec(small.shape, lambda i: (0, 0, 0))
    return pl.pallas_call(
        _write_kernel,
        name="write_out",
        grid=(blocks,),
        out_shape=(sd((dm.rows, d), F32), sd((dm.chunk, d), F32), sd((1, d), F32), sd((1, 1), F32)),
        in_specs=[some, some, half, rows],
        out_specs=(some, half, row, one),
    )(*parts, dx, small)


def solution(mesh):
    group = mesh.shape[AXIS]

    def local_step(residual, labels, loss_mask, norm_gain, table_shard):
        tokens, dim = residual.shape
        rows = table_shard.shape[0]
        dm = Dims(tokens, dim, rows, group)
        x4 = residual.reshape(16, 8, dm.chunk, dim)
        lab = labels.reshape(16, 8, 1, dm.chunk)
        msk = loss_mask.reshape(16, 8, 1, dm.chunk)
        d_embed, d_res, d_gain, loss = _run(dm, x4, table_shard, norm_gain[None, :], lab, msk)
        return loss.reshape(()), d_res, d_embed, d_gain.reshape(dim)

    return jax.shard_map(
        local_step,
        mesh=mesh,
        in_specs=(P(), P(), P(), P(), P(AXIS, None)),
        out_specs=(P(), P(AXIS, None), P(AXIS, None), P()),
        check_vma=False,
    )
```

profile of v0, /device:TPU:1, one launch (start us, length us, event | category | flops | bytes accessed | tf_op | source)
XLA Modules:
  0.0 258.7 jit_solution(10512511519145534314)
XLA Ops:
  0.6 253.2 %head.1 = (f32[128,2048]{1,0:T(8,128)}, f32[8,1,2176]{2,1,0:T(1,128)}, f32[392,2048]{1,0:T(8,128)}, f32[392,2048]{1,0:T(8,128)}, f32[392,2048]{1,0:T(8,128)}, /*...) custom-call(bf16[16,8,128,2048]{3,2,1,0:T(8,128)(2,1)} %bitcast.x4, ...), custom_call_target="tpu_custom_call" | custom-call | tf_op jit(solution)/shard_map/head/pallas_call | solution.py:898
  253.8 4.7 %write_out.1 = (f32[386,2048]{1,0:T(8,128)}, f32[128,2048]{1,0:T(8,128)}, f32[1,2048]{1,0:T(1,128)}, f32[1,1]{1,0:T(1,128)}) custom-call(f32[392,2048]{1,0:T(8,128)} %get-tuple-element.12.own, f32[392,2048]{1,0:T(8,128)} %get-tuple-element.13.ring, f32[128,2048]{1,0:T(8,128)} %get-tuple-element.14.dx, f32[8,1,2176]{2,1,0:T(1,128)} %get-tuple-element.15.small), custom_call_target="tpu_custom_call" | custom-call | tf_op jit(solution)/shard_map/write_out/pallas_call | solution.py:944
where the time goes:
time: 259 us
  Pallas kernels  258 us (100%)
    pallas_call x1, Pallas kernels, _run(): pl.pallas_call(functools.partial(_kernel, dm), name='head', out_shape=(sd...  253 us

commit v1 on v0

--- a/solution.py
+++ b/solution.py
@@ -935,7 +935,8 @@
 
 
 def _write_out(dm, parts, dx, small):
-    d, step, blocks = dm.dim, dm.ha + 8, 2
+    d, blocks = dm.dim, 4
+    step = -(-dm.pad // (8 * blocks)) * 8
     sd = jax.ShapeDtypeStruct
     some = pl.BlockSpec((step, d), lambda i: (i, 0))
     half = pl.BlockSpec((dm.chunk // blocks, d), lambda i: (i, 0))

time: 259 us -> 260 us (level)
  no operation moved by 1% of the time
where the time goes in v1:
time: 260 us
  Pallas kernels  259 us (100%)
    pallas_call x1, Pallas kernels, _run(): pl.pallas_call(functools.partial(_kernel, dm), name='head', out_shape=(sd...  253 us
    pallas_call x1, Pallas kernels, _write_out(): pl.pallas_call(_write_kernel, name='write_out', grid=(blocks,), out_shape...  5.56 us

profile of v1, /device:TPU:1, one launch (start us, length us, event | category | flops | bytes accessed | tf_op | source)
XLA Modules:
  0.0 259.5 jit_solution(16311898889831979231)
XLA Ops:
  0.6 253.2 %head.1 = (f32[128,2048]{1,0:T(8,128)}, f32[8,1,2176]{2,1,0:T(1,128)}, f32[392,2048]{1,0:T(8,128)}, f32[392,2048]{1,0:T(8,128)}, f32[392,2048]{1,0:T(8,128)}, /*...) custom-call(bf16[16,8,128,2048]{3,2,1,0:T(8,128)(2,1)} %bitcast.x4, ...), custom_call_target="tpu_custom_call" | custom-call | tf_op jit(solution)/shard_map/head/pallas_call | solution.py:898
  253.8 5.6 %write_out.1 = (f32[386,2048]{1,0:T(8,128)}, f32[128,2048]{1,0:T(8,128)}, f32[1,2048]{1,0:T(1,128)}, f32[1,1]{1,0:T(1,128)}) custom-call(f32[392,2048]{1,0:T(8,128)} %get-tuple-element.12.own, f32[392,2048]{1,0:T(8,128)} %get-tuple-element.13.ring, f32[128,2048]{1,0:T(8,128)} %get-tuple-element.14.dx, f32[8,1,2176]{2,1,0:T(1,128)} %get-tuple-element.15.small), custom_call_target="tpu_custom_call" | custom-call | tf_op jit(solution)/shard_map/write_out/pallas_call | solution.py:945
